TPU v7x, 256 devices: a whole 4x4x8 slice. The times are simulated.
256 devices in a mesh: tm: 16 (over y, x), sat: 16 (over z, core).
Axes of the slice: x: 4, y: 4, z: 8, core: 2. Of those that a mesh axis runs over, the one named last changes fastest.
Arguments:
- samples: int32 [2, 32, 8192], P(None, 'tm', 'sat'), may hold values from -1073741824 to 1073741823
- codes: int32 [48, 4092], P('sat'), may hold values from -1 to 1, as said below
- dopplers: int32 [64], replicated, may hold values from -60 to 60
Outputs:
- power: float32 [64, 48, 8192], P('tm', 'sat')
- detection: float32 [48], P('sat')
Inputs may be any that keep to these rules, and one draw needn't show every extreme that they name: `codes`: each entry is -1 or 1.
All inputs are finite; a program needn't handle non-finite values.
Results may differ from a plain program's by a relative error of at most 0.0003.
Values sent between devices are 32-bit elements.
No kernel may reach another device: no remote copies, remote signals or barrier semaphores. Data moves between devices by JAX's collectives and lax.ppermute only.
A program may use at most 64 MiB of HBM per device.

v0:
```python
import math

import jax
import jax.numpy as jnp
from jax import lax
from jax.sharding import Mesh
from jax.sharding import PartitionSpec as P

SAT = ("sat_0", "sat_1")
TM = ("tm_0", "tm_1")
TM_SAT = ("tm_0", "tm_1", "sat_0", "sat_1")


sample_scale = 2.0 ** (-29)
wrap_count = 32768


def sent_to_all(x, axis):
    copies = jnp.broadcast_to(x, (lax.axis_size(axis), *x.shape))
    return lax.all_to_all(copies, axis, split_axis=0, concat_axis=0, tiled=True)


def laid_out(parts, dim):
    dims = list(parts.shape[1:])
    dims[dim] *= parts.shape[0]
    return jnp.moveaxis(parts, 0, dim).reshape(dims)


def collect(x, axis, dim):
    parts = sent_to_all(x, axis)
    return laid_out(parts, dim)


def own_rows(running, axes):
    for axis in axes:
        running = lax.psum_scatter(running, axis, scatter_dimension=0, tiled=True)
    return running


def one_axis_at_a_time(x, axes):
    for axis in axes:
        x = lax.psum(x, axis)
    return x


def by_axis(x, axes):
    for axis in axes:
        x = lax.pmax(x, axis)
    return x


def dft_angles(outer, inner):
    sample_length = outer * inner
    rows_outer = jnp.arange(outer, dtype=jnp.int32)
    rows_inner = jnp.arange(inner, dtype=jnp.int32)
    angle_outer = jnp.mod(rows_outer[:, None] * rows_outer[None, :], outer).astype(jnp.float32) * (
        2.0 * math.pi / outer
    )
    angle_twist = jnp.mod(rows_outer[:, None] * rows_inner[None, :], sample_length).astype(
        jnp.float32
    ) * (2.0 * math.pi / sample_length)
    angle_inner = jnp.mod(rows_inner[:, None] * rows_inner[None, :], inner).astype(jnp.float32) * (
        2.0 * math.pi / inner
    )
    return (angle_outer, angle_twist, angle_inner)


def unit_pair(angles, direction):
    return (jnp.cos(angles), direction * jnp.sin(angles))


def product_complex(pattern, left_pair, right_pair):

    def contract(first_operand, right_term):
        return jnp.einsum(pattern, first_operand, right_term, precision=lax.Precision.HIGHEST)

    return (
        contract(left_pair[0], right_pair[0]) - contract(left_pair[1], right_pair[1]),
        contract(left_pair[0], right_pair[1]) + contract(left_pair[1], right_pair[0]),
    )


def twisted(pair, factor):
    return (pair[0] * factor[0] - pair[1] * factor[1], pair[0] * factor[1] + pair[1] * factor[0])


def forward_dft(pair):
    sample_length = pair[0].shape[-1]
    inner = min(128, sample_length)
    outer = sample_length // inner
    leading = pair[0].shape[:-1]
    shaped = (pair[0].reshape(leading + (outer, inner)), pair[1].reshape(leading + (outer, inner)))
    angle_outer, angle_twist, angle_inner = dft_angles(outer, inner)
    sectioned = product_complex("kn,...nm->...km", unit_pair(angle_outer, -1.0), shaped)
    sectioned = twisted(sectioned, unit_pair(angle_twist, -1.0))
    return product_complex("...kn,nm->...km", sectioned, unit_pair(angle_inner, -1.0))


def inverse_dft(pair):
    outer = pair[0].shape[-2]
    inner = pair[0].shape[-1]
    angle_outer, angle_twist, angle_inner = dft_angles(outer, inner)
    sectioned = product_complex("...kn,nm->...km", pair, unit_pair(angle_inner, 1.0))
    sectioned = twisted(sectioned, unit_pair(angle_twist, 1.0))
    return product_complex("nk,...km->...nm", unit_pair(angle_outer, 1.0), sectioned)


def replica_rows(code_rows, sample_length):
    chip_count = code_rows.shape[1]
    offsets = jnp.arange(sample_length, dtype=jnp.int32)
    chip_index = offsets * chip_count // sample_length
    halves = jnp.mod(offsets * (2 * chip_count) // sample_length, 2)
    sign_rows = (1 - 2 * halves).astype(jnp.float32)
    return jnp.take(code_rows, chip_index, axis=1).astype(jnp.float32) * sign_rows[None, :]


def to_float(block_ints):
    return (
        block_ints[0].astype(jnp.float32) * sample_scale,
        block_ints[1].astype(jnp.float32) * sample_scale,
    )


def block_powers(signal_pair, bin_rows, code_spectra):
    signal_real, signal_imag = signal_pair
    sample_length = signal_real.shape[-1]
    offsets = jnp.arange(sample_length, dtype=jnp.int32)
    rotation_angles = jnp.mod(bin_rows[:, None] * offsets[None, :], wrap_count).astype(
        jnp.float32
    ) * (2.0 * math.pi / wrap_count)
    cosine = jnp.cos(rotation_angles)[:, None, :]
    sine_part = jnp.sin(rotation_angles)[:, None, :]
    wiped_record = (
        signal_real[None] * cosine + signal_imag[None] * sine_part,
        signal_imag[None] * cosine - signal_real[None] * sine_part,
    )
    spectra = forward_dft(wiped_record)
    code_real = code_spectra[0][None, None]
    code_imag = code_spectra[1][None, None]
    spec_real = spectra[0][:, :, None]
    spec_imag = spectra[1][:, :, None]
    cross = (
        spec_real * code_real + spec_imag * code_imag,
        spec_imag * code_real - spec_real * code_imag,
    )
    lagged = inverse_dft(cross)
    powers = (lagged[0] * lagged[0] + lagged[1] * lagged[1]) * (1.0 / float(sample_length) ** 3)
    return powers.reshape(powers.shape[:3] + (sample_length,))


def shards(samples, codes, dopplers):
    sample_length = samples.shape[2] * lax.axis_size(SAT)
    segment = samples.astype(jnp.float32) * sample_scale
    local_power = jnp.sum(segment * segment)
    own_blocks = collect(samples, SAT, 2)
    replicas = replica_rows(codes, sample_length)
    code_spectra = forward_dft((replicas, jnp.zeros_like(replicas)))
    segment_tally = own_blocks.shape[1] * lax.axis_size(TM)
    dop_rows = dopplers.shape[0] // lax.axis_size(TM)
    own_pair = to_float(own_blocks)

    def one_group(cluster_frequencies):
        return jnp.sum(block_powers(own_pair, cluster_frequencies, code_spectra), axis=1)

    summed = lax.map(one_group, dopplers.reshape(-1, dop_rows))
    integrated = own_rows(summed.reshape((dop_rows * lax.axis_size(TM),) + summed.shape[2:]), TM)
    power_map = integrated * (1.0 / segment_tally)
    peak_local = jnp.max(power_map, axis=(0, 2))
    power_sum = one_axis_at_a_time(local_power, TM_SAT)
    peak_value = by_axis(peak_local, TM)
    average_energy = power_sum / float(segment_tally * sample_length)
    detection = peak_value / jnp.maximum(average_energy, 0.25)
    return (power_map, detection)


def solution(mesh):
    torus = Mesh(mesh.devices.reshape(4, 4, 8, 2), ("tm_0", "tm_1", "sat_0", "sat_1"))
    placed = (P(None, TM, SAT), P(SAT, None), P())
    return jax.shard_map(
        shards, mesh=torus, in_specs=placed, out_specs=(P(TM, SAT, None), P(SAT)), check_vma=False
    )
```

profile of v0, /device:TPU:32, one launch (start us, length us, event | category | flops | bytes accessed | tf_op | source)
XLA Modules:
  0.0 460.9 jit_solution(4087396947991783430)
XLA Ops:
  7.2 1.4 broadcast_in_dim.22
  8.6 8.6 %all-to-all-start = ((s32[16,2,2,512]{3,2,1,0:T(2,128)}), s32[16,2,2,512]{3,2,1,0:T(2,128)S(1)}, u32[]{:S(2)}, u32[]{:S(2)}) async-start(s32[16,2,2,512]{3,2,1,0:T(2,128)} %broadcast_in_dim.22), calls=%async_computation | async-start | bytes 262144 | tf_op jit(solution)/shard_map/all_to_all | solution.py:20
  18.0 1.5 copy.12
  19.5 27.7 %gather_fusion = s32[8192,3]{1,0:T(8,128)} fusion(s32[3,4092]{0,1:T(8,128)S(1)} %copy.12, s32[8192]{0:T(1024)S(1)} %broadcast_clamp_fusion), kind=kCustom, calls=%fused_computation | custom fusion | bytes 229376 | tf_op jit(solution)/shard_map/jit(_take)/gather | solution.py:114
  47.2 2.8 copy.13
  53.3 245.1 %while.13 = (s32[]{:T(128)}, f32[16,4,3,8192]{3,1,0,2:T(4,128)}, f32[2,8192]{1,0:T(2,128)S(1)}, s32[16,4]{1,0:T(8,128)S(1)}, f32[2,8192]{1,0:T(2,128)S(1)}, /*in...) while((s32[]{:T(128)}, f32[16,4,3,8192]{3,1,0,2:T(4,128)}, f32[2,8192]{1,0:T(2,128)S(1)}, ...), condition=%wide.region_2.3_spmd, body=%wide.region_0.2_spmd.sunk | while | flops 2427191296 | bytes 28607112 | solution.py:165
  63.3 1.1 fusion.352
  66.5 1.1 fusion.353
  80.7 1.1 fusion.351
  81.8 1.1 fusion.353
  96.0 1.1 fusion.351
  97.1 1.1 fusion.353
  109.2 1.1 fusion.352
  112.4 1.1 fusion.353
  124.5 1.1 fusion.352
  127.7 1.1 fusion.353
  139.9 1.1 fusion.352
  143.0 1.1 fusion.353
  155.2 1.1 fusion.352
  158.4 1.1 fusion.353
  172.6 1.1 fusion.351
  173.7 1.1 fusion.353
  187.9 1.1 fusion.351
  189.0 1.1 fusion.353
  203.2 1.1 fusion.351
  204.3 1.1 fusion.353
  218.5 1.1 fusion.351
  219.6 1.1 fusion.353
  233.8 1.1 fusion.351
  234.9 1.1 fusion.353
  247.0 1.1 fusion.352
  250.2 1.1 fusion.353
  265.4 1.1 fusion.353
  279.7 1.1 fusion.351
  280.8 1.1 fusion.353
  295.0 1.1 fusion.351
  296.0 1.1 fusion.353
  297.3 1.1 copy_dynamic-update-slice_fusion.2
  298.4 7.7 %reshape.331 = f32[64,3,8192]{2,0,1:T(8,128)} reshape(f32[16,4,3,8192]{3,1,0,2:T(4,128)} %get-tuple-element.125) | data formatting | bytes 12582912 | tf_op jit(solution)/shard_map/reshape | solution.py:166
  306.1 67.9 %reduce-scatter.3.cloned.1.call-done = f32[16,3,8192]{2,0,1:T(8,128)} async-done(((f32[64,3,8192]{2,0,1:T(8,128)}), f32[16,3,8192]{2,0,1:T(8,128)}) %reduce-scatter.3.cloned.1.call-update) | async-done | bytes 1572880 | tf_op jit(solution)/shard_map/reduce_scatter | solution.py:36
  374.7 9.2 %psum.28 = f32[]{:T(128)} all-reduce(f32[]{:T(128)} %multiply_reduce_fusion), channel_id=1, replica_groups=mesh['tm_0'=4,'tm_1'=4,'sat_0'=8,'sat_1'=2] {'tm_0'}, use_global_device_ids=true, to_apply=%region_9.10 | all-reduce | flops 1 | bytes 8 | tf_op jit(solution)/shard_map/psum | solution.py:42
  383.8 11.5 %psum.29 = f32[]{:T(128)} all-reduce(f32[]{:T(128)} %psum.28), channel_id=1, replica_groups=mesh['tm_0'=4,'tm_1'=4,'sat_0'=8,'sat_1'=2] {'tm_1'}, use_global_device_ids=true, to_apply=%region_10.11 | all-reduce | flops 1 | bytes 8 | tf_op jit(solution)/shard_map/psum | solution.py:42
  395.3 16.7 %psum.30 = f32[]{:T(128)} all-reduce(f32[]{:T(128)} %psum.29), channel_id=1, replica_groups=mesh['tm_0'=4,'tm_1'=4,'sat_0'=8,'sat_1'=2] {'sat_0'}, use_global_device_ids=true, to_apply=%region_11.12 | all-reduce | flops 1 | bytes 8 | tf_op jit(solution)/shard_map/psum | solution.py:42
  412.0 3.1 psum.31
  416.9 14.8 %all-reduce.3.cloned.1.call-done = f32[16,3,8192]{2,0,1:T(8,128)} async-done(((f32[16,3,8192]{2,0,1:T(8,128)}), f32[16,3,8192]{2,0,1:T(8,128)}) %all-reduce.3.cloned.1.call-update) | async-done | bytes 1572880
  431.7 2.0 fusion.293
  433.7 10.4 %pmax.14 = f32[3]{0:T(128)S(1)} all-reduce(f32[3]{0:T(128)S(1)} %get-tuple-element.140), channel_id=1, replica_groups=mesh['tm_0'=4,'tm_1'=4,'sat_0'=8,'sat_1'=2] {'tm_0'}, use_global_device_ids=true, to_apply=%region_6.7 | all-reduce | flops 3 | bytes 24 | tf_op jit(solution)/shard_map/pmax | solution.py:48
  444.1 9.4 %pmax.15 = f32[3]{0:T(128)S(1)} all-reduce(f32[3]{0:T(128)S(1)} %pmax.14), channel_id=1, replica_groups=mesh['tm_0'=4,'tm_1'=4,'sat_0'=8,'sat_1'=2] {'tm_1'}, use_global_device_ids=true, to_apply=%region_7.8 | all-reduce | flops 3 | bytes 24 | tf_op jit(solution)/shard_map/pmax | solution.py:48
  (382 shorter events, 213.7 us)
Async XLA Ops:
  7.2 45.5 %copy-start.1 = (s32[64]{0:T(128)S(1)}, s32[64]{0:T(128)}, u32[]{:S(2)}) copy-start(s32[64]{0:T(128)} %param.7) | copy-start | bytes 772
  8.6 44.7 %all-to-all-start = ((s32[16,2,2,512]{3,2,1,0:T(2,128)}), s32[16,2,2,512]{3,2,1,0:T(2,128)S(1)}, u32[]{:S(2)}, u32[]{:S(2)}) async-start(s32[16,2,2,512]{3,2,1,0:T(2,128)} %broadcast_in_dim.22), calls=%async_computation | async-start | bytes 262144 | tf_op jit(solution)/shard_map/all_to_all | solution.py:20
  17.2 356.9 %reduce-scatter.3.cloned.1.call-start = ((), (), s32[]{:S(2)}) async-start(), calls=%async_computation.2 | async-start | bytes 7864320 | tf_op jit(solution)/shard_map/reduce_scatter | solution.py:36
  306.0 68.0 %copy-start = (s32[2,2,512]{2,1,0:T(2,128)S(1)}, s32[2,2,512]{2,1,0:T(2,128)}, u32[]{:S(2)}) copy-start(s32[2,2,512]{2,1,0:T(2,128)} %param.5) | copy-start | bytes 24580
  306.0 109.0 %copy-start.2 = (u32[256]{0:T(256)S(1)}, u32[256]{0:T(256)}, u32[]{:S(2)}) copy-start(u32[256]{0:T(256)} %constant.275) | copy-start | bytes 3076
  306.1 125.6 %all-reduce.3.cloned.1.call-start = ((), (), s32[]{:S(2)}) async-start(), calls=%async_computation.3 | async-start | bytes 3145728
Sparse Core Ops, SparseCore 0:
  306.2 67.7 reduce-scatter.2
  376.4 55.2 all-reduce.2
where the time goes:
time: 461 us
  matrix products  212 us (46%)
  waiting for transfers between devices  82.7 us (18%)
  local copies, waits for them, and re-layouts  61.2 us (13%)
  blocking collectives  60.2 us (13%)
  other arithmetic  17.9 us (4%)
  between operations  15.5 us (3%)
  starting transfers between devices  8.66 us (2%)
    dot_general x264, matrix products, contract(): jnp.einsum(pattern, first_operand, right_term, precision=lax.Precision.HI...  212 us
    reduce_scatter x1, waiting for transfers between devices, own_rows(): running = lax.psum_scatter(running, axis, scatter_dimension=0, tiled=True)  67.9 us
    psum x4, blocking collectives, one_axis_at_a_time(): x = lax.psum(x, axis)  40.4 us
    gather x2, local copies, waits for them, and re-layouts, replica_rows(): jnp.take(code_rows, chip_index, axis=1).astype(jnp.float32)  30.5 us
    pmax x2, blocking collectives, by_axis(): x = lax.pmax(x, axis)  19.8 us
    dynamic_update_slice x16, local copies, waits for them, and re-layouts, shards(): summed = lax.map(one_group, dopplers.reshape(-1, dop_rows))  16.4 us
    unnamed x3, waiting for transfers between devices  14.8 us
    cos x16, other arithmetic, block_powers(): cosine = jnp.cos(rotation_angles)[:, None, :]  9.48 us
  transfers between devices with their start and end apart: 3, of which 2 were waited for; matrix products, arithmetic and copies ran while one was open for 8% of the time, Pallas kernels for 0%

commit v1 on v0

v1 whole, which is shorter than its diff:
```python
import functools, math
import jax, jax.numpy as jnp, numpy as np
from jax import lax
from jax.experimental import pallas as pl
from jax.experimental.pallas import tpu as pltpu

HI, LANE = 64, 128
F32, BF16 = jnp.float32, jnp.bfloat16

def turns(num, den, sign):
    a = (num % den).astype(np.float64) * (2 * np.pi / den)
    return np.cos(a), sign * np.sin(a)

def two(x):
    hi = x.astype(jnp.bfloat16)
    return hi, (x - hi.astype(np.float64)).astype(jnp.bfloat16)

def right_matrix(sign, order=None):
    k = np.arange(LANE)
    rows = k if order is None else order
    c, s = turns(rows[:, None] * k[None, :], LANE, sign)
    hi, lo = two(np.block([[c, s], [-s, c]]))
    return np.concatenate([hi, hi, lo], axis=0)

def left_block(c, s):
    return np.block([[c, -s], [s, c]])

def left_matrix(sign):
    k = np.arange(HI)
    c, s = turns(k[:, None] * k[None, :], HI, sign)
    hi, lo = two(left_block(c, s))
    return np.concatenate([np.concatenate([hi, hi], 1), np.concatenate([lo, lo], 1)], 0)

def twist(sign, order=None):
    cols = np.arange(LANE) if order is None else order
    c, s = turns(np.arange(HI)[:, None] * cols[None, :], HI * LANE, sign)
    return np.stack([c, s]).astype(np.float32)

ORDER = np.concatenate([np.arange(0, LANE, 2), np.arange(1, LANE, 2)])

def pieces(x):
    hi = x.astype(BF16)
    return hi, (x - hi.astype(F32)).astype(BF16)

def dot(a, b):
    return jnp.dot(a, b, preferred_element_type=F32)

def joined(x_ref, i, p, b):
    low = lax.broadcasted_iota(jnp.int32, (8, 8, LANE), 1) < 4
    y, x = i // 4, i % 4
    first, second = x_ref[0, x, y, :, p], x_ref[1, x, y, :, p]
    if b == 0:
        second = pltpu.roll(second, 4, 1)
    else:
        first = pltpu.roll(first, 4, 1)
    return jnp.where(low, first, second).reshape(HI, LANE)

def main_kernel(x_ref, lf_ref, tf_ref, m_ref, c_ref, a_ref, t_ref, li_ref, out_ref, pw_ref,
                xw_ref, l_ref, y_ref, z_ref, *, nb, ns, nf):
    out_ref[...] = jnp.zeros_like(out_ref)
    R = nf * 2 * HI
    def body(i, tally):
        for b in range(2):
            for p in range(2):
                v = joined(x_ref, i, p, b).astype(F32) * (2.0 ** -29)
                tally = tally + jnp.sum((v * v).reshape(8, 8, 128), axis=0)
                hi, lo = pieces(v)
                xw_ref[p * HI:(p + 1) * HI, b * LANE:(b + 1) * LANE] = hi
                xw_ref[(2 + p) * HI:(3 + p) * HI, b * LANE:(b + 1) * LANE] = lo
        xw = xw_ref[...]
        def put(ref, row, re, im):
            for p, v in ((0, re), (1, im)):
                hi, lo = pieces(v)
                cols = slice(p * LANE, (p + 1) * LANE)
                ref[row:row + HI, p * LANE:(p + 1) * LANE] = hi
                ref[row:row + HI, 256 + p * LANE:256 + (p + 1) * LANE] = lo
        for f in range(nf):
            g = dot(lf_ref[f * 256:(f + 1) * 256], xw)
            for b in range(2):
                cols = slice(b * LANE, (b + 1) * LANE)
                zr = g[0:64, cols] + g[128:192, cols]
                zi = g[64:128, cols] + g[192:256, cols]
                tr, ti = tf_ref[f, 0], tf_ref[f, 1]
                put(l_ref, (f * 2 + b) * HI, zr * tr - zi * ti, zr * ti + zi * tr)
        spec = dot(l_ref[...], m_ref[0:512]) + dot(l_ref[:, 0:256], m_ref[512:768])
        y_ref[...] = spec
        for s in range(ns):
            cr, ci = c_ref[s, 0], c_ref[s, 1]
            for fb in range(nf * 2):
                xr = y_ref[fb * HI:(fb + 1) * HI, 0:LANE]
                xi = y_ref[fb * HI:(fb + 1) * HI, LANE:2 * LANE]
                put(l_ref, fb * HI, xr * cr + xi * ci, xi * cr - xr * ci)
            g = dot(l_ref[...], a_ref[0:512]) + dot(l_ref[:, 0:256], a_ref[512:768])
            tr, ti = t_ref[0], t_ref[1]
            for f in range(nf):
                for b in range(2):
                    rows = slice((f * 2 + b) * HI, (f * 2 + b + 1) * HI)
                    zr, zi = g[rows, 0:LANE], g[rows, LANE:2 * LANE]
                    col = slice((f * 2 + b) * LANE, (f * 2 + b + 1) * LANE)
                    for p, v in ((0, zr * tr - zi * ti), (1, zr * ti + zi * tr)):
                        hi, lo = pieces(v)
                        z_ref[p * HI:(p + 1) * HI, col] = hi
                        z_ref[(2 + p) * HI:(3 + p) * HI, col] = lo
            for f in range(0, nf, 2):
                r = dot(li_ref[...], z_ref[:, f * 256:(f + 2) * 256])
                for ff in range(2):
                    tot = None
                    for b in range(2):
                        col = slice((ff * 2 + b) * LANE, (ff * 2 + b + 1) * LANE)
                        re = r[0:64, col] + r[128:192, col]
                        im = r[64:128, col] + r[192:256, col]
                        v = re * re + im * im
                        tot = v if tot is None else tot + v
                    o = (f + ff) * ns + s
                    out_ref[o] += tot
        return tally
    tally = lax.fori_loop(0, nb // 2, body, jnp.zeros((8, 128), F32))
    pw_ref[0] = jnp.zeros((8, LANE), F32) + jnp.sum(tally)
    for s in range(ns):
        best = None
        for f in range(nf):
            v = out_ref[f * ns + s] * (2.0 ** -44)
            out_ref[f * ns + s] = v
            best = v if best is None else jnp.maximum(best, v)
        pw_ref[1 + s] = jnp.zeros((8, LANE), F32) + jnp.max(best)

def main_call(x, lf, tf, m, c, a, t, li):
    nb, ns, nf = 2 * x.shape[1] * x.shape[2], c.shape[0], tf.shape[0]
    return pl.pallas_call(
        functools.partial(main_kernel, nb=nb, ns=ns, nf=nf),
        out_shape=(jax.ShapeDtypeStruct((nf * ns, HI, LANE), F32), jax.ShapeDtypeStruct((1 + ns, 8, LANE), F32)),
        scratch_shapes=[pltpu.VMEM((256, 256), BF16), pltpu.VMEM((nf * 2 * HI, 512), BF16),
                        pltpu.VMEM((nf * 2 * HI, 256), F32), pltpu.VMEM((256, nf * 256), BF16)],
    )(x, lf, tf, m, c, a, t, li)

def code_kernel(r_ref, l_ref, t_ref, m_ref, c_ref, s_ref):
    ns = r_ref.shape[0]
    for s in range(ns):
        g = dot(l_ref[...], r_ref[s])
        zr = g[0:64] + g[128:192]
        zi = g[64:128] + g[192:256]
        tr, ti = t_ref[0], t_ref[1]
        for p, v in ((0, zr * tr - zi * ti), (1, zr * ti + zi * tr)):
            hi, lo = pieces(v)
            s_ref[s * HI:(s + 1) * HI, p * LANE:(p + 1) * LANE] = hi
            s_ref[s * HI:(s + 1) * HI, 256 + p * LANE:256 + (p + 1) * LANE] = lo
            s_ref[s * HI:(s + 1) * HI, 512 + p * LANE:512 + (p + 1) * LANE] = hi
    g = dot(s_ref[...], m_ref[...])
    for s in range(ns):
        for p in range(2):
            c_ref[s, p] = g[s * HI:(s + 1) * HI, p * LANE:(p + 1) * LANE]

def code_call(rep, l0, t0, m0):
    ns = rep.shape[0]
    return pl.pallas_call(code_kernel, out_shape=jax.ShapeDtypeStruct((ns, 2, HI, LANE), F32),
        scratch_shapes=[pltpu.VMEM((ns * HI, 768), BF16)])(rep, l0, t0, m0)

def replica(codes):
    ns = codes.shape[0]
    seg = codes.reshape(ns, 4, 1023)
    even = jnp.concatenate([seg[:, :, 0:1], seg], axis=2).reshape(ns, HI, 64)
    odd = jnp.concatenate([seg[:, :, 0:512], seg[:, :, 511:1023]], axis=2).reshape(ns, HI, 64)
    n = LANE * np.arange(HI)[:, None] + ORDER[None, :]
    sign = 1 - 2 * ((n * 8184 // 8192) % 2)
    return (jnp.concatenate([even, odd], axis=2) * jnp.asarray(sign, jnp.int32)).astype(BF16)

def code_spectra(codes):
    k = np.arange(HI)
    c, s = turns(k[:, None] * k[None, :], HI, -1.0)
    hi, lo = two(np.concatenate([c, s], 0))
    l0 = np.concatenate([hi, lo], 0)
    return code_call(replica(codes), jnp.asarray(l0), jnp.asarray(twist(-1.0, ORDER)), jnp.asarray(right_matrix(-1.0, ORDER)))

def doppler_tables(dop):
    nf = dop.shape[0]
    k = jnp.arange(HI, dtype=jnp.int32)
    num = jnp.mod(4 * k[:, None] * k[None, :] + dop[:, None, None] * k, 256).astype(F32) * (2 * math.pi / 256)
    c, s = jnp.cos(num), -jnp.sin(num)
    blk = jnp.concatenate([jnp.concatenate([c, -s], 2), jnp.concatenate([s, c], 2)], 1)
    top = lax.reduce_precision(blk, 8, 7)
    hi, lo = top.astype(BF16), (blk - top).astype(BF16)
    lf = jnp.concatenate([jnp.concatenate([hi, hi], 2), jnp.concatenate([lo, lo], 2)], 1)
    n = jnp.arange(LANE, dtype=jnp.int32)
    num = jnp.mod(4 * k[:, None] * n[None, :] + dop[:, None, None] * n, 32768).astype(F32) * (2 * math.pi / 32768)
    tf = jnp.stack([jnp.cos(num), -jnp.sin(num)], 1)
    return lf.reshape(nf * 256, 256), tf

from jax.sharding import Mesh
from jax.sharding import PartitionSpec as P

TM, SAT = ("y", "x"), ("z", "c")


def spread(x, axis):
    copies = jnp.broadcast_to(x, (lax.axis_size(axis), *x.shape))
    return lax.all_to_all(copies, axis, split_axis=0, concat_axis=0, tiled=True)


def shards(samples, codes, dopplers):
    nf = dopplers.shape[0] // lax.axis_size(TM)
    dop = lax.dynamic_slice_in_dim(dopplers, lax.axis_index(TM) * nf, nf)
    x = samples.reshape(2, 8, LANE)
    for axis in ("z", "y", "x", "c"):
        x = spread(x, axis)
    lf, tf = doppler_tables(dop)
    c = code_spectra(codes)
    power, facts = main_call(x, lf, tf, jnp.asarray(right_matrix(-1.0)), c, jnp.asarray(right_matrix(1.0)),
                             jnp.asarray(twist(1.0)), jnp.asarray(left_matrix(1.0)))
    peak = jnp.max(spread(facts[1:, 0, 0], TM), axis=0)
    mean = facts[0, 0, 0] * (1.0 / 262144)
    return power.reshape(nf, -1, HI * LANE), peak / jnp.maximum(mean, 0.25)


def solution(mesh):
    torus = Mesh(mesh.devices.reshape(4, 4, 8, 2), ("y", "x", "z", "c"))
    return jax.shard_map(
        shards, mesh=torus, in_specs=(P(None, TM, SAT), P(SAT, None), P()),
        out_specs=(P(TM, SAT, None), P(SAT)), check_vma=False,
    )
```

time: 461 us -> 128 us (0.28)
  matrix products: 212 us -> 0 us
  waiting for transfers between devices: 82.7 us -> 24.3 us
  Pallas kernels: 0 us -> 58.1 us
  blocking collectives: 60.2 us -> 6.29 us
  local copies, waits for them, and re-layouts: 61.2 us -> 10.1 us
  between operations: 15.5 us -> 1.36 us
  other arithmetic: 17.9 us -> 5.17 us
  starting transfers between devices: 8.66 us -> 20.7 us
    dot_general x264 -> x0, matrix products: 212 us -> none  [contract(): jnp.einsum(pattern, first_operand, right_term, precision=lax.Precision.HI...]
    reduce_scatter x1 -> x0, waiting for transfers between devices: 67.9 us -> none  [own_rows(): running = lax.psum_scatter(running, axis, scatter_dimension=0, tiled=True)]
    pallas_call x0 -> x2, Pallas kernels: none -> 58.1 us  [the longest x1 55.9 us: main_call(): pl.pallas_call(functools.partial(main_kernel, nb=nb, ns=ns, nf=nf), out_s...]
    psum x4 -> x0, blocking collectives: 40.4 us -> none  [one_axis_at_a_time(): x = lax.psum(x, axis)]
    gather x2 -> x0, local copies, waits for them, and re-layouts: 30.5 us -> none  [replica_rows(): jnp.take(code_rows, chip_index, axis=1).astype(jnp.float32)]
    all_to_all x1 -> x4, waiting for transfers between devices: 0.01 us -> 24.3 us  [spread(): return lax.all_to_all(copies, axis, split_axis=0, concat_axis=0, tiled=True)]
    pmax x2 -> x0, blocking collectives: 19.8 us -> none  [by_axis(): x = lax.pmax(x, axis)]
    dynamic_update_slice x16 -> x0, local copies, waits for them, and re-layouts: 16.4 us -> none  [shards(): summed = lax.map(one_group, dopplers.reshape(-1, dop_rows))]
  transfers between devices with their start and end apart: 3 -> 4, of which waited for: 2 -> 4; matrix products, arithmetic and copies ran while one was open for 8% -> 5% of each run, Pallas kernels for 0% -> 2%
where the time goes in v1:
time: 128 us; the launch traced here: 126 us
  Pallas kernels  58.1 us (45%)
  waiting for transfers between devices  24.3 us (19%)
  starting transfers between devices  20.7 us (16%)
  local copies, waits for them, and re-layouts  10.1 us (8%)
  blocking collectives  6.29 us (5%)
  other arithmetic  5.17 us (4%)
  between operations  1.36 us (1%)
    pallas_call x1, Pallas kernels, main_call(): pl.pallas_call(functools.partial(main_kernel, nb=nb, ns=ns, nf=nf), out_s...  55.9 us
    all_to_all x4, waiting for transfers between devices, spread(): return lax.all_to_all(copies, axis, split_axis=0, concat_axis=0, tiled=True)  24.3 us
    all_to_all x4, starting transfers between devices, spread(): return lax.all_to_all(copies, axis, split_axis=0, concat_axis=0, tiled=True)  20.7 us
    all_to_all x1, blocking collectives, spread(): return lax.all_to_all(copies, axis, split_axis=0, concat_axis=0, tiled=True)  6.29 us
    broadcast_in_dim x5, local copies, waits for them, and re-layouts, spread(): copies = jnp.broadcast_to(x, (lax.axis_size(axis), *x.shape))  3.26 us
  transfers between devices with their start and end apart: 4, of which 4 were waited for; matrix products, arithmetic and copies ran while one was open for 5% of the time, Pallas kernels for 2%

profile of v1, /device:TPU:32, one launch (start us, length us, event | category | flops | bytes accessed | tf_op | source)
XLA Modules:
  0.0 126.0 jit_solution(1333117765940428815)
XLA Ops:
  0.6 0.7 reshape.169
  1.3 0.6 broadcast_in_dim.12
  2.0 8.6 %all-to-all-start = ((s32[8,2,8,128]{3,2,1,0:T(8,128)}), s32[8,2,8,128]{3,2,1,0:T(8,128)S(1)}, u32[]{:S(2)}, u32[]{:S(2)}) async-start(s32[8,2,8,128]{3,2,1,0:T(8,128)} %broadcast_in_dim.12), calls=%async_computation | async-start | bytes 131072 | tf_op jit(solution)/shard_map/all_to_all | solution.py:196
  10.5 0.9 reshape.171
  11.5 0.1 fusion.12
  11.6 0.7 dynamic_slice.3
  12.3 0.1 iota_multiply_fusion.2
  12.4 0.1 iota_multiply_fusion
  12.5 0.1 reshape.173
  12.6 0.1 pad_add_fusion
  12.7 0.1 reshape.172
  12.8 0.5 fusion.8
  13.3 1.5 %fusion.7.r_ref = bf16[3,64,128]{2,1,0:T(8,128)(2,1)} fusion(s32[3,64,64]{2,1,0:T(8,128)S(1)} %reshape.173, s32[3,64,64]{2,1,0:T(8,128)S(1)} %reshape.172, s32[64,128]{1,0:T(8,128)} %constant.73.clone), kind=kLoop, calls=%fused_computation.24 | loop fusion | flops 73728 | bytes 180224 | tf_op jit(solution)/shard_map/convert_element_type | solution.py:165
  14.8 2.2 %shard_map.122.c_ref = f32[3,2,64,128]{3,2,1,0:T(8,128)} custom-call(bf16[3,64,128]{2,1,0:T(8,128)(2,1)} %fusion.7.r_ref, bf16[256,64]{1,0:T(8,128)(2,1)} %constant.74.clone.l_ref, f32[2,64,128]{2,1,0:T(8,128)} %constant.75.clone.t_ref, bf16[768,256]{1,0:T(8,128)(2,1)} %constant.76.clone.m_ref), custom_call_target="tpu_custom_call" | custom-call | tf_op jit(solution)/shard_map/pallas_call | solution.py:155
  17.0 0.5 all-to-all-done
  17.5 0.7 broadcast_in_dim.13
  18.2 4.5 %all-to-all-start.1 = ((s32[4,8,2,8,128]{4,3,2,1,0:T(8,128)}), s32[4,8,2,8,128]{4,3,2,1,0:T(8,128)S(1)}, u32[]{:S(2)}, u32[]{:S(2)}) async-start(s32[4,8,2,8,128]{4,3,2,1,0:T(8,128)} %broadcast_in_dim.13), calls=%async_computation.1 | async-start | bytes 524288 | tf_op jit(solution)/shard_map/all_to_all | solution.py:196
  22.6 0.1 iota_multiply_fusion.3
  22.7 6.6 %all-to-all-done.1 = s32[4,8,2,8,128]{4,3,2,1,0:T(8,128)S(1)} async-done(((s32[4,8,2,8,128]{4,3,2,1,0:T(8,128)}), s32[4,8,2,8,128]{4,3,2,1,0:T(8,128)S(1)}, u32[]{:S(2)}, u32[]{:S(2)}) %all-to-all-start.1) | async-done | bytes 262176 | tf_op jit(solution)/shard_map/all_to_all | solution.py:196
  29.3 1.1 broadcast_in_dim.14
  30.4 4.3 %all-to-all-start.2 = ((s32[4,4,8,2,8,128]{5,4,3,2,1,0:T(8,128)}), s32[4,4,8,2,8,128]{5,4,3,2,1,0:T(8,128)S(1)}, u32[]{:S(2)}, u32[]{:S(2)}) async-start(s32[4,4,8,2,8,128]{5,4,3,2,1,0:T(8,128)} %broadcast_in_dim.14), calls=%async_computation.2 | async-start | bytes 2097152 | tf_op jit(solution)/shard_map/all_to_all | solution.py:196
  34.7 0.7 pad_maximum_fusion.tf_ref
  35.4 0.1 iota_multiply_fusion.1
  35.5 0.5 fusion.9
  36.0 0.1 reduce-precision_convert_fusion
  36.2 0.8 maximum_maximum_fusion
  37.0 10.3 %all-to-all-done.2 = s32[4,4,8,2,8,128]{5,4,3,2,1,0:T(8,128)S(1)} async-done(((s32[4,4,8,2,8,128]{5,4,3,2,1,0:T(8,128)}), s32[4,4,8,2,8,128]{5,4,3,2,1,0:T(8,128)S(1)}, u32[]{:S(2)}, u32[]{:S(2)}) %all-to-all-start.2) | async-done | bytes 1048608 | tf_op jit(solution)/shard_map/all_to_all | solution.py:196
  47.3 0.2 broadcast_in_dim.15
  47.6 6.3 %all_to_all.26.x_ref = s32[2,4,4,8,2,8,128]{6,5,4,3,2,1,0:T(8,128)} all-to-all(s32[2,4,4,8,2,8,128]{6,5,4,3,2,1,0:T(8,128)S(1)} %broadcast_in_dim.15), channel_id=1, replica_groups=mesh['y'=4,'x'=4,'z'=8,'c'=2] {'c'}, dimensions={0} | all-to-all | bytes 4194304 | tf_op jit(solution)/shard_map/all_to_all | solution.py:196
  53.9 55.9 %shard_map.123 = (f32[12,64,128]{2,1,0:T(8,128)}, f32[4,8,128]{2,1,0:T(8,128)}) custom-call(s32[2,4,4,8,2,8,128]{6,5,4,3,2,1,0:T(8,128)} %all_to_all.26.x_ref, bf16[1024,256]{1,0:T(8,128)(2,1)} %bitcast.2, f32[4,2,64,128]{3,2,1,0:T(8,128)} %pad_maximum_fusion.tf_ref, bf16[768,256]{1,0:T(8,128)(2,1)} %constant.77.clone.m_ref, ...), custom_call_target="tpu_custom_call" | custom-call | tf_op jit(solution)/shard_map/pallas_call | solution.py:129
  109.8 0.8 slice_reduce_fusion
  110.6 1.2 slice.19
  111.8 1.2 reshape.174
  113.0 1.0 copy.19
  114.0 0.6 broadcast_in_dim.33
  114.6 3.4 %all-to-all-start.4 = ((f32[16,1,3]{2,1,0:T(1,128)}), f32[16,1,3]{2,1,0:T(1,128)S(1)}, u32[]{:S(2)}, u32[]{:S(2)}) async-start(f32[16,1,3]{2,1,0:T(1,128)} %broadcast_in_dim.33), calls=%async_computation.4 | async-start | bytes 16384 | tf_op jit(solution)/shard_map/all_to_all | solution.py:196
  118.6 6.9 %all-to-all-done.4 = f32[16,1,3]{2,1,0:T(1,128)S(1)} async-done(((f32[16,1,3]{2,1,0:T(1,128)}), f32[16,1,3]{2,1,0:T(1,128)S(1)}, u32[]{:S(2)}, u32[]{:S(2)}) %all-to-all-start.4) | async-done | bytes 224 | tf_op jit(solution)/shard_map/all_to_all | solution.py:196
  125.5 0.5 broadcast_divide_fusion
  (4 shorter events, 0.0 us)
Async XLA Ops:
  2.0 15.5 %all-to-all-start = ((s32[8,2,8,128]{3,2,1,0:T(8,128)}), s32[8,2,8,128]{3,2,1,0:T(8,128)S(1)}, u32[]{:S(2)}, u32[]{:S(2)}) async-start(s32[8,2,8,128]{3,2,1,0:T(8,128)} %broadcast_in_dim.12), calls=%async_computation | async-start | bytes 131072 | tf_op jit(solution)/shard_map/all_to_all | solution.py:196
  18.2 11.1 %all-to-all-start.1 = ((s32[4,8,2,8,128]{4,3,2,1,0:T(8,128)}), s32[4,8,2,8,128]{4,3,2,1,0:T(8,128)S(1)}, u32[]{:S(2)}, u32[]{:S(2)}) async-start(s32[4,8,2,8,128]{4,3,2,1,0:T(8,128)} %broadcast_in_dim.13), calls=%async_computation.1 | async-start | bytes 524288 | tf_op jit(solution)/shard_map/all_to_all | solution.py:196
  30.4 16.9 %all-to-all-start.2 = ((s32[4,4,8,2,8,128]{5,4,3,2,1,0:T(8,128)}), s32[4,4,8,2,8,128]{5,4,3,2,1,0:T(8,128)S(1)}, u32[]{:S(2)}, u32[]{:S(2)}) async-start(s32[4,4,8,2,8,128]{5,4,3,2,1,0:T(8,128)} %broadcast_in_dim.14), calls=%async_computation.2 | async-start | bytes 2097152 | tf_op jit(solution)/shard_map/all_to_all | solution.py:196
  114.6 10.9 %all-to-all-start.4 = ((f32[16,1,3]{2,1,0:T(1,128)}), f32[16,1,3]{2,1,0:T(1,128)S(1)}, u32[]{:S(2)}, u32[]{:S(2)}) async-start(f32[16,1,3]{2,1,0:T(1,128)} %broadcast_in_dim.33), calls=%async_computation.4 | async-start | bytes 16384 | tf_op jit(solution)/shard_map/all_to_all | solution.py:196
